TPU v7x, 32 devices: a whole 2x2x4 slice. The times are simulated.
32 devices in a mesh: dp: 4 (over y, x), blk: 8 (over z, core).
Axes of the slice: x: 2, y: 2, z: 4, core: 2. Of those that a mesh axis runs over, the one named last changes fastest.
Arguments:
- particles: float32 [1024, 1024], P('blk'), may hold values from -14 to 14
- data_rows: bfloat16 [16384, 1024], P('dp'), may hold values from -0.1875 to 0.1875
- labels: int32 [16384], P('dp'), may hold values from 0 to 1
Outputs:
- descent: float32 [1024, 1024], P('blk')
All inputs are finite; a program needn't handle non-finite values.
Results may differ from a plain program's by a relative error of at most 0.0045.
Values may be sent and summed in bfloat16 or wider, within the bound.
A program may use at most 64 MiB of HBM per device.

v0:
```python
import jax
import jax.numpy as jnp
from jax import lax
from jax.sharding import PartitionSpec as P

prior_var = 4.0


def pair_sums(left_x, left_s, right_x, right_s, inv_band):
    feature_count = left_x.shape[1]
    left_xf = left_x.astype(jnp.float32)
    left_sf = left_s.astype(jnp.float32)
    right_xf = right_x.astype(jnp.float32)
    right_sf = right_s.astype(jnp.float32)
    left_norm = jnp.sum(left_xf * left_xf, axis=1)
    right_norm = jnp.sum(right_xf * right_xf, axis=1)
    left_sx = jnp.sum(left_sf * left_xf, axis=1)
    right_sx = jnp.sum(right_sf * right_xf, axis=1)
    gram_xx = jnp.einsum("id,jd->ij", left_x, right_x, preferred_element_type=jnp.float32)
    gram_ss = jnp.einsum("id,jd->ij", left_s, right_s, preferred_element_type=jnp.float32)
    cross_dot = jnp.einsum(
        "id,jd->ij",
        jnp.concatenate([left_x, left_s], axis=1),
        jnp.concatenate([right_s, right_x], axis=1),
        preferred_element_type=jnp.float32,
    )
    distance = left_norm[:, None] + right_norm[None, :] - 2.0 * gram_xx
    kernel = jnp.exp(-0.5 * inv_band * distance)
    bracket = (
        gram_ss
        + inv_band * (left_sx[:, None] - cross_dot + right_sx[None, :])
        + feature_count * inv_band
        - inv_band * inv_band * distance
    )
    weighted_kernel = kernel * bracket
    kernel_sum = jnp.sum(kernel, axis=1)
    weighted_sum = jnp.sum(weighted_kernel, axis=1)
    both_rows = jnp.dot(
        kernel.astype(jnp.bfloat16),
        jnp.concatenate([right_x, right_s], axis=1),
        preferred_element_type=jnp.float32,
    )
    kernel_x = both_rows[:, :feature_count]
    kernel_s = both_rows[:, feature_count:]
    weighted_x = jnp.dot(
        weighted_kernel.astype(jnp.bfloat16), right_x, preferred_element_type=jnp.float32
    )
    return (kernel_sum, weighted_sum, kernel_x, kernel_s, weighted_x)


def forces(left_x, left_s, sums, inv_band, particle_count):
    kernel_sum, weighted_sum, kernel_x, kernel_s, weighted_x = sums
    left_xf = left_x.astype(jnp.float32)
    left_sf = left_s.astype(jnp.float32)
    spread = kernel_sum[:, None] * left_xf - kernel_x
    score_force = (kernel_s + inv_band * spread) / particle_count
    place_force = (
        -inv_band * (weighted_sum[:, None] * left_xf - weighted_x)
        + inv_band * (kernel_sum[:, None] * left_sf - kernel_s)
        - 2.0 * inv_band * inv_band * spread
    ) / particle_count
    return (score_force, place_force)


def empty_sums(rows_count, feature_count):
    flat_zero = jnp.zeros((rows_count,), jnp.float32)
    wide_zero = jnp.zeros((rows_count, feature_count), jnp.float32)
    return (flat_zero, flat_zero, wide_zero, wide_zero, wide_zero)


def pair_folder(left_x, left_s, inv_band, running, pieces):
    pair_parts = pair_sums(left_x, left_s, pieces[0], pieces[1], inv_band)
    return jax.tree.map(jnp.add, running, pair_parts)


def shards(particles, data_rows, labels):
    block_rows, feature_count = particles.shape
    groups_count = lax.axis_size("dp")
    particle_count = block_rows * lax.axis_size("blk")
    inv_band = 1.0 / feature_count
    x_low = particles.astype(jnp.bfloat16)
    logits = jnp.einsum("pd,md->pm", x_low, data_rows, preferred_element_type=jnp.float32)
    probability = jax.nn.sigmoid(logits)
    residual = (labels.astype(jnp.float32)[None, :] - probability).astype(jnp.bfloat16)
    curvature = probability * (1.0 - probability)
    partial_score = jnp.dot(residual, data_rows, preferred_element_type=jnp.float32)
    scores = lax.psum(partial_score, "dp") - particles / prior_var
    s_low = scores.astype(jnp.bfloat16)
    share_rows = block_rows // groups_count
    offset = lax.axis_index("dp") * share_rows
    left_x = lax.dynamic_slice_in_dim(x_low, offset, share_rows, 0)
    left_s = lax.dynamic_slice_in_dim(s_low, offset, share_rows, 0)
    sums = pair_folder(
        left_x,
        left_s,
        inv_band,
        empty_sums(share_rows, feature_count),
        (
            lax.all_gather(x_low, "blk", axis=0, tiled=True),
            lax.all_gather(s_low, "blk", axis=0, tiled=True),
        ),
    )
    score_force, place_force = forces(left_x, left_s, sums, inv_band, particle_count)
    full_force = lax.all_gather(score_force, "dp", axis=0, tiled=True)
    own_place = lax.dynamic_update_slice_in_dim(
        jnp.zeros((block_rows, feature_count), jnp.float32), place_force, offset, 0
    )
    projected = jnp.einsum(
        "pd,md->pm", full_force.astype(jnp.bfloat16), data_rows, preferred_element_type=jnp.float32
    )
    weighted_rows = (curvature * projected).astype(jnp.bfloat16)
    data_term = jnp.dot(weighted_rows, data_rows, preferred_element_type=jnp.float32)
    summed = lax.psum(data_term - own_place, "dp")
    return summed + full_force / prior_var


def solution(mesh):
    placed = (P("blk", None), P("dp", None), P("dp"))
    return jax.shard_map(
        shards, mesh=mesh, in_specs=placed, out_specs=P("blk", None), check_vma=False
    )
```

profile of v0, /device:TPU:0, one launch (start us, length us, event | category | flops | bytes accessed | tf_op | source)
XLA Modules:
  0.0 181.4 jit_solution(16980919114636974199)
XLA Ops:
  7.4 0.0 all-reduce.3.cloned.1.call-start
  7.4 0.7 convert_element_type.42
  8.1 1.1 convert_element_type.38
  9.2 0.0 copy-start
  9.2 6.5 %fusion.3 = f32[128,4096]{1,0:T(8,128)S(1)} fusion(bf16[128,1024]{1,0:T(8,128)(2,1)S(1)} %convert_element_type.38, bf16[4096,1024]{1,0:T(8,128)(2,1)} %param.4), kind=kOutput, calls=%fused_computation.7 | convolution fusion | flops 1075314688 | bytes 10747904 | tf_op jit(solution)/shard_map/pd,md->pm/dot_general | solution.py:82
  15.7 1.3 copy-done.2
  17.0 2.1 %fusion.32 = f32[128,1024]{1,0:T(8,128)} fusion(bf16[4096,1024]{1,0:T(8,128)(2,1)S(1)} %copy-done, f32[128,4096]{1,0:T(8,128)S(1)} %fusion.3, f32[4096]{0:T(1024)S(1)} %convert_element_type.42), kind=kOutput, calls=%fused_computation.36 | convolution fusion | flops 1074790400 | bytes 11026432 | tf_op jit(solution)/shard_map/dot_general | solution.py:86
  19.1 0.0 all-reduce.3.cloned.1.call-update
  19.2 0.0 all-gather.3.cloned.1.call-start
  19.2 0.5 all-gather.3.cloned.1.call-update
  19.7 0.0 all-gather.5.cloned.1.call-start
  19.8 47.6 %all-reduce.3.cloned.1.call-done = f32[128,1024]{1,0:T(8,128)} async-done(((f32[128,1024]{1,0:T(8,128)}), f32[128,1024]{1,0:T(8,128)}) %all-reduce.3.cloned.1.call-update) | async-done | bytes 524304 | tf_op jit(solution)/shard_map/psum | solution.py:87
  67.4 1.8 subtract_convert_fusion.2
  69.2 0.0 all-gather.5.cloned.1.call-update
  69.2 0.0 all-reduce.5.cloned.1.call-start
  69.3 1.0 fusion.40
  70.3 0.0 all-gather.3.cloned.1.call-done
  70.3 28.1 %all-gather.5.cloned.1.call-done = bf16[1024,1024]{1,0:T(8,128)(2,1)} async-done(((bf16[128,1024]{1,0:T(8,128)(2,1)}), bf16[1024,1024]{1,0:T(8,128)(2,1)}) %all-gather.5.cloned.1.call-update) | async-done | bytes 2097168 | tf_op jit(solution)/shard_map/all_gather | solution.py:100
  98.4 3.1 %fusion.5 = (f32[1024]{0:T(1024)S(1)}, f32[1024]{0:T(1024)S(1)}) fusion(bf16[1024,1024]{1,0:T(8,128)(2,1)} %all-gather.3.cloned.1.call-done, bf16[1024,1024]{1,0:T(8,128)(2,1)} %all-gather.5.cloned.1.call-done), kind=kLoop, calls=%fused_computation.9 | loop fusion | flops 6289408 | bytes 4202496 | tf_op jit(solution)/shard_map/reduce_sum | solution.py:18
  101.6 0.8 fusion.44
  102.4 0.7 copy-done.3
  103.1 0.8 fusion.6
  103.9 0.1 add_multiply_fusion
  104.0 10.0 %all_gather.11 = f32[128,1024]{1,0:T(8,128)S(1)} all-gather(f32[32,1024]{1,0:T(8,128)S(1)} %add_multiply_fusion), channel_id=1, replica_groups=mesh['dp'=4,'blk'=8] {'dp'}, dimensions={0}, use_global_device_ids=true | all-gather | bytes 655360 | tf_op jit(solution)/shard_map/all_gather | solution.py:104
  114.0 1.3 fusion.29
  115.4 0.8 fusion.53
  116.2 0.1 broadcast_in_dim.2
  116.3 0.5 fusion.18
  116.8 11.2 %convolution_subtract_fusion = f32[128,1024]{1,0:T(8,128)} fusion(f32[128,1024]{1,0:T(8,128)S(1)} %fusion.18, bf16[4096,1024]{1,0:T(8,128)(2,1)} %param.4, f32[128,4096]{1,0:T(8,128)} %copy-done.2, f32[128,1024]{1,0:T(8,128)S(1)} %all_gather.11), kind=kOutput, calls=%fused_computation.20 | convolution fusion | flops 2149842944 | bytes 12058624 | tf_op jit(solution)/shard_map/dot_general | solution.py:112
  128.0 0.0 all-reduce.5.cloned.1.call-update
  128.1 44.0 %all-reduce.5.cloned.1.call-done = f32[128,1024]{1,0:T(8,128)} async-done(((f32[128,1024]{1,0:T(8,128)}), f32[128,1024]{1,0:T(8,128)}) %all-reduce.5.cloned.1.call-update) | async-done | bytes 524304 | tf_op jit(solution)/shard_map/psum | solution.py:113
  172.0 1.9 %multiply_add_fusion = f32[128,1024]{1,0:T(8,128)} fusion(f32[128,1024]{1,0:T(8,128)} %all-reduce.5.cloned.1.call-done, f32[128,1024]{1,0:T(8,128)S(1)} %all_gather.11), kind=kLoop, calls=%fused_computation.38 | loop fusion | flops 262144 | bytes 1572864 | tf_op jit(solution)/shard_map/add | solution.py:114
  (9 shorter events, 0.0 us)
Async XLA Ops:
  7.4 60.0 %all-reduce.3.cloned.1.call-start = ((), (), s32[]{:S(2)}) async-start(), calls=%async_computation.1 | async-start | bytes 1048576 | tf_op jit(solution)/shard_map/psum | solution.py:87
  9.2 6.5 %copy-start.5 = (bf16[128,1024]{1,0:T(8,128)(2,1)}, bf16[128,1024]{1,0:T(8,128)(2,1)S(1)}, u32[]{:S(2)}) copy-start(bf16[128,1024]{1,0:T(8,128)(2,1)S(1)} %convert_element_type.38) | copy-start | bytes 786436
  9.2 7.9 %copy-start = (bf16[4096,1024]{1,0:T(8,128)(2,1)S(1)}, bf16[4096,1024]{1,0:T(8,128)(2,1)}, u32[]{:S(2)}) copy-start(bf16[4096,1024]{1,0:T(8,128)(2,1)} %param.4) | copy-start | bytes 25165828
  15.7 1.4 copy-start.2
  17.0 50.4 %copy-start.4 = (f32[128,1024]{1,0:T(8,128)S(1)}, f32[128,1024]{1,0:T(8,128)}, u32[]{:S(2)}) copy-start(f32[128,1024]{1,0:T(8,128)} %param.3) | copy-start | bytes 1572868
  19.2 51.2 %all-gather.3.cloned.1.call-start = ((), (), s32[]{:S(2)}) async-start(), calls=%async_computation | async-start | bytes 2359296 | tf_op jit(solution)/shard_map/all_gather | solution.py:99
  19.7 78.7 %all-gather.5.cloned.1.call-start = ((), (), s32[]{:S(2)}) async-start(), calls=%async_computation.2 | async-start | bytes 2359296 | tf_op jit(solution)/shard_map/all_gather | solution.py:100
  69.2 102.8 %all-reduce.5.cloned.1.call-start = ((), (), s32[]{:S(2)}) async-start(), calls=%async_computation.3 | async-start | bytes 1048576 | tf_op jit(solution)/shard_map/psum | solution.py:113
  70.3 31.2 %copy-start.1 = (bf16[1024,1024]{1,0:T(8,128)(2,1)S(1)}, bf16[1024,1024]{1,0:T(8,128)(2,1)}, u32[]{:S(2)}) copy-start(bf16[1024,1024]{1,0:T(8,128)(2,1)} %all-gather.3.cloned.1.call-done) | copy-start | bytes 6291460
  101.5 1.6 copy-start.3
Sparse Core Ops, SparseCore 0:
  19.3 48.0 all-reduce.2
  128.2 43.7 all-reduce.4
Sparse Core Ops, SparseCore 1:
  21.2 31.8 all-gather.2
  69.3 29.0 all-gather.4
where the time goes:
time: 182 us; the launch traced here: 181 us
  waiting for transfers between devices  120 us (66%)
  matrix products  24.2 us (13%)
  between operations  15 us (8%)
  blocking collectives  10 us (5%)
  other arithmetic  9.71 us (5%)
  local copies, waits for them, and re-layouts  2.14 us (1%)
    psum x1, waiting for transfers between devices, shards(): scores = lax.psum(partial_score, 'dp') - particles / prior_var  47.6 us
    psum x1, waiting for transfers between devices, shards(): summed = lax.psum(data_term - own_place, 'dp')  44 us
    all_gather x1, waiting for transfers between devices, shards(): lax.all_gather(s_low, 'blk', axis=0, tiled=True)  28.1 us
    dot_general x1, matrix products, shards(): jnp.dot(weighted_rows, data_rows, preferred_element_type=jnp.float32)  11.2 us
    all_gather x1, blocking collectives, shards(): full_force = lax.all_gather(score_force, 'dp', axis=0, tiled=True)  10 us
    dot_general x1, matrix products, shards(): jnp.einsum('pd,md->pm', x_low, data_rows, preferred_element_type=jnp.floa...  6.47 us
  transfers between devices with their start and end apart: 4, of which 3 were waited for; matrix products, arithmetic and copies ran while one was open for 2% of the time, Pallas kernels for 0%

commit v1 on v0

--- a/solution.py
+++ b/solution.py
@@ -110,7 +110,8 @@
     )
     weighted_rows = (curvature * projected).astype(jnp.bfloat16)
     data_term = jnp.dot(weighted_rows, data_rows, preferred_element_type=jnp.float32)
-    summed = lax.psum(data_term - own_place, "dp")
+    _treat_map = lambda unit: jnp.sum(jax.lax.all_gather(unit, "dp"), axis=0)
+    summed = _treat_map(data_term - own_place)
     return summed + full_force / prior_var
 
 

time: 182 us -> 172 us (0.945)
  waiting for transfers between devices: 120 us -> 110 us
    psum x1 -> x0, waiting for transfers between devices: 44 us -> none  [shards(): summed = lax.psum(data_term - own_place, 'dp')]
    all_gather x0 -> x1, waiting for transfers between devices: none -> 33.8 us  [shards(): _treat_map = lambda unit: jnp.sum(jax.lax.all_gather(unit, 'dp'), axis=0)]
where the time goes in v1:
time: 172 us
  waiting for transfers between devices  110 us (64%)
  matrix products  24.2 us (14%)
  between operations  15 us (9%)
  other arithmetic  10.5 us (6%)
  blocking collectives  10 us (6%)
  local copies, waits for them, and re-layouts  2.14 us (1%)
    psum x1, waiting for transfers between devices, shards(): scores = lax.psum(partial_score, 'dp') - particles / prior_var  47.6 us
    all_gather x1, waiting for transfers between devices, shards(): _treat_map = lambda unit: jnp.sum(jax.lax.all_gather(unit, 'dp'), axis=0)  33.8 us
    all_gather x1, waiting for transfers between devices, shards(): lax.all_gather(s_low, 'blk', axis=0, tiled=True)  28.1 us
    dot_general x1, matrix products, shards(): jnp.dot(weighted_rows, data_rows, preferred_element_type=jnp.float32)  11.2 us
    all_gather x1, blocking collectives, shards(): full_force = lax.all_gather(score_force, 'dp', axis=0, tiled=True)  10 us
    dot_general x1, matrix products, shards(): jnp.einsum('pd,md->pm', x_low, data_rows, preferred_element_type=jnp.floa...  6.47 us
  transfers between devices with their start and end apart: 4, of which 3 were waited for; matrix products, arithmetic and copies ran while one was open for 2% of the time, Pallas kernels for 0%

profile of v1, /device:TPU:0, one launch (start us, length us, event | category | flops | bytes accessed | tf_op | source)
XLA Modules:
  0.0 171.9 jit_solution(755957474403363872)
XLA Ops:
  7.4 0.7 convert_element_type.42
  8.1 1.1 convert_element_type.38
  9.2 0.0 copy-start
  9.2 6.5 %fusion.3 = f32[128,4096]{1,0:T(8,128)S(1)} fusion(bf16[128,1024]{1,0:T(8,128)(2,1)S(1)} %convert_element_type.38, bf16[4096,1024]{1,0:T(8,128)(2,1)} %param.4), kind=kOutput, calls=%fused_computation.7 | convolution fusion | flops 1075314688 | bytes 10747904 | tf_op jit(solution)/shard_map/pd,md->pm/dot_general | solution.py:82
  15.7 1.3 copy-done.2
  17.0 2.1 %fusion.32 = f32[128,1024]{1,0:T(8,128)} fusion(bf16[4096,1024]{1,0:T(8,128)(2,1)S(1)} %copy-done, f32[128,4096]{1,0:T(8,128)S(1)} %fusion.3, f32[4096]{0:T(1024)S(1)} %convert_element_type.42), kind=kOutput, calls=%fused_computation.36 | convolution fusion | flops 1074790400 | bytes 11026432 | tf_op jit(solution)/shard_map/dot_general | solution.py:86
  19.1 0.0 all-reduce.2.cloned.1.call-update
  19.2 0.0 all-gather.5.cloned.1.call-start
  19.2 0.5 all-gather.5.cloned.1.call-update
  19.7 0.0 all-gather.7.cloned.1.call-start
  19.8 47.6 %all-reduce.2.cloned.1.call-done = f32[128,1024]{1,0:T(8,128)} async-done(((f32[128,1024]{1,0:T(8,128)}), f32[128,1024]{1,0:T(8,128)}) %all-reduce.2.cloned.1.call-update) | async-done | bytes 524304 | tf_op jit(solution)/shard_map/psum | solution.py:87
  67.4 1.8 %subtract_convert_fusion.2 = bf16[128,1024]{1,0:T(8,128)(2,1)} fusion(f32[128,1024]{1,0:T(8,128)} %all-reduce.2.cloned.1.call-done, f32[128,1024]{1,0:T(8,128)S(1)} %copy-done.4), kind=kLoop, calls=%fused_computation.39 | loop fusion | flops 393216 | bytes 1310720 | tf_op jit(solution)/shard_map/convert_element_type | solution.py:88
  69.2 0.0 all-gather.7.cloned.1.call-update
  69.2 0.0 all-gather.9.cloned.1.call-start
  69.3 1.0 fusion.40
  70.3 0.0 all-gather.5.cloned.1.call-done
  70.3 28.1 %all-gather.7.cloned.1.call-done = bf16[1024,1024]{1,0:T(8,128)(2,1)} async-done(((bf16[128,1024]{1,0:T(8,128)(2,1)}), bf16[1024,1024]{1,0:T(8,128)(2,1)}) %all-gather.7.cloned.1.call-update) | async-done | bytes 2097168 | tf_op jit(solution)/shard_map/all_gather | solution.py:100
  98.4 3.1 %fusion.5 = (f32[1024]{0:T(1024)S(1)}, f32[1024]{0:T(1024)S(1)}) fusion(bf16[1024,1024]{1,0:T(8,128)(2,1)} %all-gather.5.cloned.1.call-done, bf16[1024,1024]{1,0:T(8,128)(2,1)} %all-gather.7.cloned.1.call-done), kind=kLoop, calls=%fused_computation.9 | loop fusion | flops 6289408 | bytes 4202496 | tf_op jit(solution)/shard_map/reduce_sum | solution.py:18
  101.6 0.8 fusion.44
  102.4 0.7 copy-done.3
  103.1 0.8 fusion.6
  103.9 0.1 add_multiply_fusion
  104.0 10.0 %all_gather.17 = f32[128,1024]{1,0:T(8,128)S(1)} all-gather(f32[32,1024]{1,0:T(8,128)S(1)} %add_multiply_fusion), channel_id=1, replica_groups=mesh['dp'=4,'blk'=8] {'dp'}, dimensions={0}, use_global_device_ids=true | all-gather | bytes 655360 | tf_op jit(solution)/shard_map/all_gather | solution.py:104
  114.0 1.3 fusion.29
  115.4 0.8 fusion.53
  116.2 0.1 broadcast_in_dim.2
  116.3 0.5 fusion.18
  116.8 11.2 %convolution_subtract_fusion = f32[128,1024]{1,0:T(8,128)} fusion(f32[128,1024]{1,0:T(8,128)S(1)} %fusion.18, bf16[4096,1024]{1,0:T(8,128)(2,1)} %param.4, f32[128,4096]{1,0:T(8,128)} %copy-done.2, f32[128,1024]{1,0:T(8,128)S(1)} %all_gather.17), kind=kOutput, calls=%fused_computation.20 | convolution fusion | flops 2149842944 | bytes 12058624 | tf_op jit(solution)/shard_map/dot_general | solution.py:112
  128.0 0.0 all-gather.9.cloned.1.call-update
  128.1 33.8 %all-gather.9.cloned.1.call-done = f32[512,1024]{1,0:T(8,128)} async-done(((f32[128,1024]{1,0:T(8,128)}), f32[512,1024]{1,0:T(8,128)}) %all-gather.9.cloned.1.call-update) | async-done | bytes 2097168 | tf_op jit(solution)/shard_map/all_gather | solution.py:113
  161.8 1.8 %reduce_sum.69 = f32[128,1024]{1,0:T(8,128)S(1)} reduce(f32[4,128,1024]{2,1,0:T(8,128)} %bitcast.12, f32[]{:T(128)} %constant.7.clone.1), dimensions={0}, to_apply=%region_7.0 | reduce | flops 393216 | bytes 2621444 | tf_op jit(solution)/shard_map/reduce_sum | solution.py:113
  163.6 0.9 multiply_add_fusion
  (10 shorter events, 0.0 us)
Async XLA Ops:
  7.4 60.0 %all-reduce.2.cloned.1.call-start = ((), (), s32[]{:S(2)}) async-start(), calls=%async_computation.1 | async-start | bytes 1048576 | tf_op jit(solution)/shard_map/psum | solution.py:87
  9.2 6.5 %copy-start.5 = (bf16[128,1024]{1,0:T(8,128)(2,1)}, bf16[128,1024]{1,0:T(8,128)(2,1)S(1)}, u32[]{:S(2)}) copy-start(bf16[128,1024]{1,0:T(8,128)(2,1)S(1)} %convert_element_type.38) | copy-start | bytes 786436
  9.2 7.9 %copy-start = (bf16[4096,1024]{1,0:T(8,128)(2,1)S(1)}, bf16[4096,1024]{1,0:T(8,128)(2,1)}, u32[]{:S(2)}) copy-start(bf16[4096,1024]{1,0:T(8,128)(2,1)} %param.4) | copy-start | bytes 25165828
  15.7 1.4 copy-start.2
  17.0 50.4 %copy-start.4 = (f32[128,1024]{1,0:T(8,128)S(1)}, f32[128,1024]{1,0:T(8,128)}, u32[]{:S(2)}) copy-start(f32[128,1024]{1,0:T(8,128)} %param.3) | copy-start | bytes 1572868
  19.2 51.2 %all-gather.5.cloned.1.call-start = ((), (), s32[]{:S(2)}) async-start(), calls=%async_computation | async-start | bytes 2359296 | tf_op jit(solution)/shard_map/all_gather | solution.py:99
  19.7 78.7 %all-gather.7.cloned.1.call-start = ((), (), s32[]{:S(2)}) async-start(), calls=%async_computation.2 | async-start | bytes 2359296 | tf_op jit(solution)/shard_map/all_gather | solution.py:100
  69.2 92.6 %all-gather.9.cloned.1.call-start = ((), (), s32[]{:S(2)}) async-start(), calls=%async_computation.3 | async-start | bytes 2621440 | tf_op jit(solution)/shard_map/all_gather | solution.py:113
  70.3 31.2 %copy-start.1 = (bf16[1024,1024]{1,0:T(8,128)(2,1)S(1)}, bf16[1024,1024]{1,0:T(8,128)(2,1)}, u32[]{:S(2)}) copy-start(bf16[1024,1024]{1,0:T(8,128)(2,1)} %all-gather.5.cloned.1.call-done) | copy-start | bytes 6291460
  101.5 1.6 copy-start.3
Sparse Core Ops, SparseCore 0:
  19.3 48.0 all-reduce.1
  128.2 33.5 all-gather.8
Sparse Core Ops, SparseCore 1:
  21.2 31.8 all-gather.4
  69.3 29.0 all-gather.6
